TPU v7x, 512 devices: a whole 4x8x8 slice. The times are simulated.
512 devices in a mesh: front: 8 (over y), row: 8 (over z), col: 8 (over x, core).
Axes of the slice: x: 4, y: 8, z: 8, core: 2. Of those that a mesh axis runs over, the one named last changes fastest.
Arguments:
- pivot: float32 [8, 512, 512], P('front', ('row', 'col')), may hold values from -1 to 8
- col_ut: bfloat16 [8, 8, 96, 512], P('front', 'row', None, 'col'), may hold values from -6 to 6
- col_vt: bfloat16 [8, 8, 96, 512], P('front', 'row', None, 'col'), may hold values from -0.25 to 0.25
- col_rank: int32 [8, 8], P('front', 'row'), may hold values from 32 to 96
- row_ut: bfloat16 [8, 8, 96, 512], P('front', 'col', None, 'row'), may hold values from -6 to 6
- row_vt: bfloat16 [8, 8, 96, 512], P('front', 'col', None, 'row'), may hold values from -0.625 to 0.625
- row_rank: int32 [8, 8], P('front', 'col'), may hold values from 32 to 96
- cb_ut: bfloat16 [8, 8, 8, 96, 512], P('front', 'row', 'col'), may hold values from -6 to 6
- cb_vt: bfloat16 [8, 8, 8, 96, 512], P('front', 'row', 'col'), may hold values from -0.625 to 0.625
- cb_rank: int32 [8, 8, 8], P('front', 'row', 'col'), may hold values from 32 to 96
- parent_map: int32 [8, 8], P('front'), may hold values from 0 to 15, as said below
Outputs:
- parent_tiles: bfloat16 [8, 16, 8, 512, 512], P('front', 'row', 'col')
Inputs may be any that keep to these rules, and one draw needn't show every extreme that they name: `parent_map`: for every front the entries are distinct; entry 0 is 8, and 0 and 15 both appear.
All inputs are finite; a program needn't handle non-finite values.
Results may differ from a plain program's by a relative error of at most 0.0062.
Values may be sent and summed in bfloat16 or wider, within the bound.
No kernel may reach another device: no remote copies, remote signals or barrier semaphores. Data moves between devices by JAX's collectives and lax.ppermute only.
A program may use at most 64 MiB of HBM per device.

v0:
```python
import jax
import jax.numpy as jnp
from jax import lax
from jax.sharding import PartitionSpec as P

NS_ITERS = 2
HIGH = lax.Precision.HIGHEST


def in_order(blocks, dim):
    blocks = jnp.moveaxis(blocks, 0, dim)
    shape = blocks.shape
    return blocks.reshape(*shape[:dim], shape[dim] * shape[dim + 1], *shape[dim + 2 :])


def copy_for_each(x, axis):
    copies = jnp.broadcast_to(x, (lax.axis_size(axis), *x.shape))
    return lax.all_to_all(copies, axis, split_axis=0, concat_axis=0, tiled=True)


def gather_directly(x, axis, dim):
    return in_order(copy_for_each(x, axis), dim)


def gather_turned(arrays, axis, dims):
    turned = [jnp.moveaxis(a, dim, 0) for a, dim in zip(arrays, dims)]
    widths = [t[0].size for t in turned]
    both = jnp.concatenate([t.reshape(-1, w) for t, w in zip(turned, widths)], axis=1)
    result = lax.all_gather(both, axis, axis=0, tiled=True)
    blocks = jnp.split(result, [sum(widths[:k]) for k in range(1, len(widths))], axis=1)
    return tuple(
        (
            jnp.moveaxis(b.reshape(-1, *t.shape[1:]), 0, dim)
            for b, t, dim in zip(blocks, turned, dims)
        )
    )


def sent_together(arrays, axis, dim, along):
    widths = [a.shape[along] for a in arrays]
    both = jnp.concatenate(arrays, axis=along)
    result = lax.all_gather(both, axis, axis=dim, tiled=True)
    return tuple(jnp.split(result, [sum(widths[:k]) for k in range(1, len(widths))], axis=along))


def swapped(x, axis, bit):
    return lax.ppermute(x, axis, [(i, i ^ 1 << bit) for i in range(lax.axis_size(axis))])


def ranked(factor, rank):
    levels = jnp.arange(factor.shape[-2], dtype=jnp.int32)[:, None]
    keep = levels < rank[..., None, None]
    return jnp.where(keep, factor, jnp.zeros_like(factor))


def densify(left, right):
    return jnp.einsum("ijkx,ijky->ijxy", left, right, preferred_element_type=jnp.float32).astype(
        jnp.bfloat16
    )


def selector(mapping, first, count):
    wanted = first + jnp.arange(count, dtype=jnp.int32)
    return (mapping[None, :] == wanted[:, None]).astype(jnp.bfloat16)


def fold_rows(select_rows, carry, pieces):
    results = []
    for total, piece in zip(carry, pieces):
        count = piece.shape[0]
        flat = piece.reshape(count, -1)
        moved = jnp.dot(select_rows, flat, preferred_element_type=jnp.float32).astype(jnp.bfloat16)
        results.append(moved.reshape(total.shape))
    return tuple(results)


def fold_cols(select_cols, carry, pieces):
    results = []
    for total, piece in zip(carry, pieces):
        count = piece.shape[1]
        flat = piece.reshape(piece.shape[0], count, -1)
        moved = jnp.einsum(
            "bj,ajx->abx", select_cols, flat, preferred_element_type=jnp.float32
        ).astype(jnp.bfloat16)
        results.append(moved.reshape(total.shape))
    return tuple(results)


def shards(
    pivot, col_ut, col_vt, col_rank, row_ut, row_vt, row_rank, cb_ut, cb_vt, cb_rank, parent_map
):
    whole = gather_directly(pivot[0], ("row", "col"), 0)
    eye = jnp.eye(whole.shape[0], dtype=jnp.float32)
    approx = eye / jnp.diagonal(whole)[None, :]
    for step in range(NS_ITERS):
        approx = jnp.dot(approx, 2.0 * eye - jnp.dot(whole, approx, precision=HIGH), precision=HIGH)
    column_left, column_right = gather_turned((col_ut[0], col_vt[0]), "col", (2, 2))
    column_left = ranked(column_left, col_rank[0])
    column_right = ranked(column_right, col_rank[0])
    lower = jnp.einsum(
        "atx,xy->aty", column_right.astype(jnp.float32), approx, precision=HIGH
    ).astype(jnp.bfloat16)
    upper_left, upper_right = gather_turned((row_ut[0], row_vt[0]), "row", (2, 2))
    upper_left = ranked(upper_left, row_rank[0])
    upper_right = ranked(upper_right, row_rank[0])
    core = jnp.einsum(
        "iax,jbx->ijab", lower, upper_left, preferred_element_type=jnp.float32
    ).astype(jnp.bfloat16)
    update = jnp.einsum(
        "ijab,iax->ijbx", core, column_left, preferred_element_type=jnp.float32
    ).astype(jnp.bfloat16)
    block_left = ranked(cb_ut[0], cb_rank[0])
    block_right = ranked(cb_vt[0], cb_rank[0])
    rows_here = block_left.shape[0]
    cols_here = block_left.shape[1]
    left = jnp.concatenate([block_left, -update], axis=2)
    right = jnp.concatenate([block_right, upper_right[None]], axis=2)
    parent_rows = 2 * rows_here
    select_rows = selector(parent_map[0], lax.axis_index("row") * parent_rows, parent_rows)
    select_cols = selector(parent_map[0], lax.axis_index("col") * parent_rows, parent_rows)
    factor_shape = left.shape[2:]
    empty_rows = jnp.zeros((parent_rows, cols_here) + factor_shape, jnp.bfloat16)
    rows_left, rows_right = fold_rows(
        select_rows, (empty_rows, empty_rows), sent_together((left, right), "row", 0, 1)
    )
    empty_cols = jnp.zeros((parent_rows, parent_rows) + factor_shape, jnp.bfloat16)
    both_left, both_right = fold_cols(
        select_cols, (empty_cols, empty_cols), sent_together((rows_left, rows_right), "col", 1, 0)
    )
    placed = densify(both_left, both_right)
    side = lax.axis_index("front") % 2
    mine = lax.dynamic_slice_in_dim(placed, side * cols_here, cols_here, 1)
    other = lax.dynamic_slice_in_dim(placed, (1 - side) * cols_here, cols_here, 1)
    received = swapped(other, "front", 0)
    total = mine.astype(jnp.float32) + received.astype(jnp.float32)
    return total.astype(jnp.bfloat16)[None]


def solution(mesh):
    placed = (
        P("front", ("row", "col"), None),
        P("front", "row", None, "col"),
        P("front", "row", None, "col"),
        P("front", "row"),
        P("front", "col", None, "row"),
        P("front", "col", None, "row"),
        P("front", "col"),
        P("front", "row", "col", None, None),
        P("front", "row", "col", None, None),
        P("front", "row", "col"),
        P("front", None),
    )
    return jax.shard_map(
        shards,
        mesh=mesh,
        in_specs=placed,
        out_specs=P("front", "row", "col", None, None),
        check_vma=False,
    )
```

profile of v0, /device:TPU:1, one launch (start us, length us, event | category | flops | bytes accessed | tf_op | source)
XLA Modules:
  0.0 238.1 jit_solution(16976337831034606800)
XLA Ops:
  6.5 1.8 broadcast_in_dim.49
  8.4 15.0 %all-to-all-start = ((f32[64,8,512]{2,1,0:T(8,128)}), f32[64,8,512]{2,1,0:T(8,128)S(1)}, u32[]{:S(2)}, u32[]{:S(2)}) async-start(f32[64,8,512]{2,1,0:T(8,128)} %broadcast_in_dim.49), calls=%async_computation | async-start | bytes 2097152 | tf_op jit(solution)/shard_map/all_to_all | solution.py:18
  23.5 13.7 %all_gather.13 = bf16[512,192]{1,0:T(8,128)(2,1)S(1)} all-gather(bf16[64,192]{1,0:T(8,128)(2,1)S(1)} %pad_maximum_fusion.2), channel_id=1, replica_groups=mesh['front'=8,'row'=8,'col'=8] {'col'}, dimensions={0}, use_global_device_ids=true | all-gather | bytes 221184 | tf_op jit(solution)/shard_map/all_gather | solution.py:29
  38.2 24.5 %all_gather.12 = bf16[512,192]{1,0:T(8,128)(2,1)S(1)} all-gather(bf16[64,192]{1,0:T(8,128)(2,1)S(1)} %pad_maximum_fusion.1), channel_id=1, replica_groups=mesh['front'=8,'row'=8,'col'=8] {'row'}, dimensions={0}, use_global_device_ids=true | all-gather | bytes 221184 | tf_op jit(solution)/shard_map/all_gather | solution.py:29
  64.7 4.7 %gather_fusion = f32[512]{0:T(512)S(1)} fusion(f32[512,512]{1,0:T(8,128)S(1)} %bitcast.142, s32[512]{0:T(512)S(1)} %bitcast.141), kind=kCustom, calls=%fused_computation | custom fusion | bytes 8192 | tf_op jit(solution)/shard_map/jit(diagonal)/cond/branch_0_fun/gather | solution.py:94
  69.4 1.9 select_subtract_fusion.1
  71.3 3.6 %fusion.6 = f32[512,512]{1,0:T(8,128)S(1)} fusion(f32[512,512]{0,1:T(8,128)S(1)} %select_subtract_fusion.1, f32[512]{0:T(512)S(1)} %gather_fusion), kind=kOutput, calls=%fused_computation.24 | convolution fusion | flops 1611399168 | bytes 2099200 | tf_op jit(solution)/shard_map/dot_general | solution.py:96
  74.9 3.5 %select_subtract_fusion = f32[512,512]{0,1:T(8,128)S(1)} fusion(f32[512,512]{1,0:T(8,128)S(1)} %fusion.6, f32[64,8,512]{2,1,0:T(8,128)S(1)} %all-to-all-done), kind=kOutput, calls=%fused_computation.11 | convolution fusion | flops 1611399168 | bytes 3145728 | tf_op jit(solution)/shard_map/dot_general | solution.py:96
  78.3 1.9 fusion.43
  82.2 53.2 %all-gather.3.cloned.1.call-done = bf16[8,2,192,512]{3,2,1,0:T(8,128)(2,1)} async-done(((bf16[1,2,192,512]{3,2,1,0:T(8,128)(2,1)}), bf16[8,2,192,512]{3,2,1,0:T(8,128)(2,1)}) %all-gather.3.cloned.1.call-update) | async-done | bytes 3145744 | tf_op jit(solution)/shard_map/all_gather | solution.py:42
  135.4 2.1 slice_bitcast_fusion.1
  140.6 0.9 pad_maximum_fusion
  141.6 44.9 %all-gather.5.cloned.1.call-done = bf16[4,8,192,512]{3,2,0,1:T(8,128)(2,1)} async-done(((bf16[4,1,192,512]{3,2,0,1:T(8,128)(2,1)}), bf16[4,8,192,512]{3,2,0,1:T(8,128)(2,1)}) %all-gather.5.cloned.1.call-update) | async-done | bytes 6291472 | tf_op jit(solution)/shard_map/all_gather | solution.py:42
  186.6 3.4 %fusion.40 = (bf16[2,8,192,512]{3,2,0,1:T(8,128)(2,1)S(1)}, bf16[2,8,192,512]{3,2,0,1:T(8,128)(2,1)S(1)}) fusion(bf16[4,8,192,512]{3,2,0,1:T(8,128)(2,1)} %all-gather.5.cloned.1.call-done), kind=kLoop, calls=%fused_computation.73 | loop fusion | bytes 12582912 | tf_op jit(solution)/shard_map/split | solution.py:43
  189.9 1.8 copy.31
  191.7 1.9 fusion.1
  193.6 2.4 %reshape.193 = bf16[2,2,192,512]{3,2,1,0:T(8,128)(2,1)} reshape(bf16[2,2,98304]{2,1,0:T(2,128)(2,1)} %fusion.1) | data formatting | bytes 1572864 | tf_op jit(solution)/shard_map/reshape | solution.py:85
  196.0 1.8 copy.30
  197.8 1.0 fusion
  198.8 1.4 reshape.191
  200.3 1.9 convolution_convert_fusion.4
  202.3 3.1 %collective-permute-start = (bf16[2,1,512,512]{3,2,1,0:T(8,128)(2,1)S(1)}, bf16[2,1,512,512]{3,2,1,0:T(8,128)(2,1)}, u32[]{:S(2)}, u32[]{:S(2)}) collective-permute-start(bf16[2,1,512,512]{3,2,1,0:T(8,128)(2,1)S(1)} %constant_dynamic-slice_fusion), channel_id=1, source_target_pairs={{0,64},{64,0},{128,192},{192,128},{256,320},{320,256},{384,448},{4... | collective-permute-start | bytes 3145736 | tf_op jit(solution)/shard_map/ppermute | solution.py:47
  205.5 23.3 %collective-permute-done = bf16[2,1,512,512]{3,2,1,0:T(8,128)(2,1)} collective-permute-done((bf16[2,1,512,512]{3,2,1,0:T(8,128)(2,1)S(1)}, bf16[2,1,512,512]{3,2,1,0:T(8,128)(2,1)}, u32[]{:S(2)}, u32[]{:S(2)}) %collective-permute-start) | collective-permute-done | bytes 1048608 | tf_op jit(solution)/shard_map/ppermute | solution.py:47
  228.8 2.5 %fusion.5 = bf16[1,2,1,512,512]{4,3,2,1,0:T(8,128)(2,1)} fusion(bf16[2,1,512,512]{3,2,1,0:T(8,128)(2,1)} %collective-permute-done, bf16[2,2,512,512]{3,2,1,0:T(8,128)(2,1)S(1)} %convolution_convert_fusion.4, s32[]{:T(128)S(6)} %select_n.76), kind=kLoop, calls=%fused_computation.21 | loop fusion | flops 2097152 | bytes 3145732 | tf_op jit(solution)/shard_map/broadcast_in_dim | solution.py:136
  (46 shorter events, 6.2 us)
Async XLA Ops:
  6.5 16.9 %copy-start.4 = (bf16[1,1,96,64]{2,3,1,0:T(8,128)(2,1)S(1)}, bf16[1,1,96,64]{2,3,1,0:T(8,128)(2,1)}, u32[]{:S(2)}) copy-start(bf16[1,1,96,64]{2,3,1,0:T(8,128)(2,1)} %param.12) | copy-start | bytes 36868
  6.5 16.9 %copy-start.3 = (bf16[1,1,96,64]{2,3,1,0:T(8,128)(2,1)S(1)}, bf16[1,1,96,64]{2,3,1,0:T(8,128)(2,1)}, u32[]{:S(2)}) copy-start(bf16[1,1,96,64]{2,3,1,0:T(8,128)(2,1)} %param.13) | copy-start | bytes 36868
  6.5 31.6 %copy-start.5 = (bf16[1,1,96,64]{2,3,1,0:T(8,128)(2,1)S(1)}, bf16[1,1,96,64]{2,3,1,0:T(8,128)(2,1)}, u32[]{:S(2)}) copy-start(bf16[1,1,96,64]{2,3,1,0:T(8,128)(2,1)} %param.16) | copy-start | bytes 36868
  6.5 31.6 %copy-start.6 = (bf16[1,1,96,64]{2,3,1,0:T(8,128)(2,1)S(1)}, bf16[1,1,96,64]{2,3,1,0:T(8,128)(2,1)}, u32[]{:S(2)}) copy-start(bf16[1,1,96,64]{2,3,1,0:T(8,128)(2,1)} %param.15) | copy-start | bytes 36868
  8.4 56.2 %copy-start.1 = (bf16[1,1,1,96,512]{4,3,2,1,0:T(8,128)(2,1)S(1)}, bf16[1,1,1,96,512]{4,3,2,1,0:T(8,128)(2,1)}, u32[]{:S(2)}) copy-start(bf16[1,1,1,96,512]{4,3,2,1,0:T(8,128)(2,1)} %param.18) | copy-start | bytes 294916
  8.4 56.2 %copy-start.2 = (bf16[1,1,1,96,512]{4,3,2,1,0:T(8,128)(2,1)S(1)}, bf16[1,1,1,96,512]{4,3,2,1,0:T(8,128)(2,1)}, u32[]{:S(2)}) copy-start(bf16[1,1,1,96,512]{4,3,2,1,0:T(8,128)(2,1)} %param.19) | copy-start | bytes 294916
  8.4 56.3 %all-to-all-start = ((f32[64,8,512]{2,1,0:T(8,128)}), f32[64,8,512]{2,1,0:T(8,128)S(1)}, u32[]{:S(2)}, u32[]{:S(2)}) async-start(f32[64,8,512]{2,1,0:T(8,128)} %broadcast_in_dim.49), calls=%async_computation | async-start | bytes 2097152 | tf_op jit(solution)/shard_map/all_to_all | solution.py:18
  23.4 112.1 %all-gather.3.cloned.1.call-start = ((), (), s32[]{:S(2)}) async-start(), calls=%async_computation.1 | async-start | bytes 3538944 | tf_op jit(solution)/shard_map/all_gather | solution.py:42
  81.9 104.6 %all-gather.5.cloned.1.call-start = ((), (), s32[]{:S(2)}) async-start(), calls=%async_computation.2 | async-start | bytes 7077888 | tf_op jit(solution)/shard_map/all_gather | solution.py:42
  138.4 0.9 copy-start.7
  197.8 2.5 %copy-start = (bf16[2,2,192,512]{3,2,1,0:T(8,128)(2,1)S(1)}, bf16[2,2,192,512]{3,2,1,0:T(8,128)(2,1)}, u32[]{:S(2)}) copy-start(bf16[2,2,192,512]{3,2,1,0:T(8,128)(2,1)} %reshape.193) | copy-start | bytes 2359300
  202.3 26.5 %collective-permute-start = (bf16[2,1,512,512]{3,2,1,0:T(8,128)(2,1)S(1)}, bf16[2,1,512,512]{3,2,1,0:T(8,128)(2,1)}, u32[]{:S(2)}, u32[]{:S(2)}) collective-permute-start(bf16[2,1,512,512]{3,2,1,0:T(8,128)(2,1)S(1)} %constant_dynamic-slice_fusion), channel_id=1, source_target_pairs={{0,64},{64,0},{128,192},{192,128},{256,320},{320,256},{384,448},{4... | collective-permute-start | bytes 3145736 | tf_op jit(solution)/shard_map/ppermute | solution.py:47
Sparse Core Ops, SparseCore 0:
  82.1 53.3 all-gather.2
  141.7 44.8 all-gather.4
where the time goes:
time: 239 us; the launch traced here: 238 us
  waiting for transfers between devices  121 us (51%)
  blocking collectives  38.2 us (16%)
  local copies, waits for them, and re-layouts  21.9 us (9%)
  starting transfers between devices  18.4 us (8%)
  matrix products  17.8 us (7%)
  between operations  15.7 us (7%)
  other arithmetic  4.56 us (2%)
    all_gather x2, waiting for transfers between devices, sent_together(): result = lax.all_gather(both, axis, axis=dim, tiled=True)  98.1 us
    all_gather x2, blocking collectives, gather_turned(): result = lax.all_gather(both, axis, axis=0, tiled=True)  38.2 us
    ppermute x1, waiting for transfers between devices, swapped(): lax.ppermute(x, axis, [(i, i ^ 1 << bit) for i in range(lax.axis_size(axi...  23.3 us
    all_to_all x1, starting transfers between devices, copy_for_each(): return lax.all_to_all(copies, axis, split_axis=0, concat_axis=0, tiled=True)  15 us
    split x3, local copies, waits for them, and re-layouts, sent_together(): jnp.split(result, [sum(widths[:k]) for k in range(1, len(widths))], axis=...  6.87 us
    dot_general x2, matrix products, shards(): jnp.dot(approx, 2.0 * eye - jnp.dot(whole, approx, precision=HIGH), preci...  5.44 us
    dot_general x2, matrix products, shards(): jnp.dot(whole, approx, precision=HIGH)  5.34 us
  transfers between devices with their start and end apart: 4, of which 3 were waited for; matrix products, arithmetic and copies ran while one was open for 0% of the time, Pallas kernels for 0%

commit v1 on v0

--- a/solution.py
+++ b/solution.py
@@ -26,7 +26,8 @@
     turned = [jnp.moveaxis(a, dim, 0) for a, dim in zip(arrays, dims)]
     widths = [t[0].size for t in turned]
     both = jnp.concatenate([t.reshape(-1, w) for t, w in zip(turned, widths)], axis=1)
-    result = lax.all_gather(both, axis, axis=0, tiled=True)
+    sent = jnp.stack([both] * lax.axis_size(axis))
+    result = jnp.concatenate(lax.all_to_all(sent, axis, 0, 0), axis=0)
     blocks = jnp.split(result, [sum(widths[:k]) for k in range(1, len(widths))], axis=1)
     return tuple(
         (

time: 239 us -> 243 us (1.017)
  waiting for transfers between devices: 121 us -> 144 us
  blocking collectives: 38.2 us -> 15.6 us
    all_gather x2 -> x0, blocking collectives: 38.2 us -> none  [gather_turned(): result = lax.all_gather(both, axis, axis=0, tiled=True)]
    all_to_all x1, waiting for transfers between devices: 0.01 us -> 25.4 us  [copy_for_each(): return lax.all_to_all(copies, axis, split_axis=0, concat_axis=0, tiled=True)]
    all_to_all x0 -> x1, blocking collectives: none -> 15.6 us  [gather_turned(): result = jnp.concatenate(lax.all_to_all(sent, axis, 0, 0), axis=0)]
    all_to_all x0 -> x1, starting transfers between devices: none -> 10.2 us  [gather_turned(): result = jnp.concatenate(lax.all_to_all(sent, axis, 0, 0), axis=0)]
    all_to_all x1, starting transfers between devices: 15 us -> 6.74 us  [copy_for_each(): return lax.all_to_all(copies, axis, split_axis=0, concat_axis=0, tiled=True)]
    all_gather x2, waiting for transfers between devices: 98.1 us -> 90 us  [sent_together(): result = lax.all_gather(both, axis, axis=dim, tiled=True)]
    all_to_all x0 -> x1, waiting for transfers between devices: none -> 5.64 us  [gather_turned(): result = jnp.concatenate(lax.all_to_all(sent, axis, 0, 0), axis=0)]
  transfers between devices with their start and end apart: 4 -> 5, of which waited for: 3 -> 5; matrix products, arithmetic and copies ran while one was open for 0% -> 1% of each run, Pallas kernels for 0% -> 0%
where the time goes in v1:
time: 243 us; the launch traced here: 242 us
  waiting for transfers between devices  144 us (59%)
  local copies, waits for them, and re-layouts  22.4 us (9%)
  starting transfers between devices  20.3 us (8%)
  matrix products  17.9 us (7%)
  between operations  15.7 us (6%)
  blocking collectives  15.6 us (6%)
  other arithmetic  6.07 us (2%)
    all_gather x2, waiting for transfers between devices, sent_together(): result = lax.all_gather(both, axis, axis=dim, tiled=True)  90 us
    all_to_all x1, waiting for transfers between devices, copy_for_each(): return lax.all_to_all(copies, axis, split_axis=0, concat_axis=0, tiled=True)  25.4 us
    ppermute x1, waiting for transfers between devices, swapped(): lax.ppermute(x, axis, [(i, i ^ 1 << bit) for i in range(lax.axis_size(axi...  23.3 us
    all_to_all x1, blocking collectives, gather_turned(): result = jnp.concatenate(lax.all_to_all(sent, axis, 0, 0), axis=0)  15.6 us
    all_to_all x1, starting transfers between devices, gather_turned(): result = jnp.concatenate(lax.all_to_all(sent, axis, 0, 0), axis=0)  10.2 us
    split x3, local copies, waits for them, and re-layouts, sent_together(): jnp.split(result, [sum(widths[:k]) for k in range(1, len(widths))], axis=...  6.87 us
    all_to_all x1, starting transfers between devices, copy_for_each(): return lax.all_to_all(copies, axis, split_axis=0, concat_axis=0, tiled=True)  6.74 us
    all_to_all x1, waiting for transfers between devices, gather_turned(): result = jnp.concatenate(lax.all_to_all(sent, axis, 0, 0), axis=0)  5.64 us
  transfers between devices with their start and end apart: 5, of which 5 were waited for; matrix products, arithmetic and copies ran while one was open for 1% of the time, Pallas kernels for 0%

profile of v1, /device:TPU:1, one launch (start us, length us, event | category | flops | bytes accessed | tf_op | source)
XLA Modules:
  0.0 242.3 jit_solution(15548479821128526202)
XLA Ops:
  8.1 10.2 %all-to-all-start.1 = ((bf16[8,64,192]{2,1,0:T(8,128)(2,1)}), bf16[8,64,192]{2,1,0:T(8,128)(2,1)S(1)}, u32[]{:S(2)}, u32[]{:S(2)}) async-start(bf16[8,64,192]{2,1,0:T(8,128)(2,1)} %stack.5), calls=%async_computation.1 | async-start | bytes 524288 | tf_op jit(solution)/shard_map/all_to_all | solution.py:30
  19.1 5.6 %all-to-all-done.1 = bf16[8,64,192]{2,1,0:T(8,128)(2,1)S(1)} async-done(((bf16[8,64,192]{2,1,0:T(8,128)(2,1)}), bf16[8,64,192]{2,1,0:T(8,128)(2,1)S(1)}, u32[]{:S(2)}, u32[]{:S(2)}) %all-to-all-start.1) | async-done | bytes 196640 | tf_op jit(solution)/shard_map/all_to_all | solution.py:30
  24.7 15.6 %all_to_all.15 = bf16[8,64,192]{2,1,0:T(8,128)(2,1)S(1)} all-to-all(bf16[8,64,192]{2,1,0:T(8,128)(2,1)S(1)} %stack.4), channel_id=1, replica_groups=mesh['front'=8,'row'=8,'col'=8] {'row'}, dimensions={0} | all-to-all | bytes 393216 | tf_op jit(solution)/shard_map/all_to_all | solution.py:30
  40.4 1.8 broadcast_in_dim.49
  42.2 6.7 %all-to-all-start.2 = ((f32[64,8,512]{2,1,0:T(8,128)}), f32[64,8,512]{2,1,0:T(8,128)S(1)}, u32[]{:S(2)}, u32[]{:S(2)}) async-start(f32[64,8,512]{2,1,0:T(8,128)} %broadcast_in_dim.49), calls=%async_computation.2 | async-start | bytes 2097152 | tf_op jit(solution)/shard_map/all_to_all | solution.py:18
  51.8 25.4 %all-to-all-done.2 = f32[64,8,512]{2,1,0:T(8,128)S(1)} async-done(((f32[64,8,512]{2,1,0:T(8,128)}), f32[64,8,512]{2,1,0:T(8,128)S(1)}, u32[]{:S(2)}, u32[]{:S(2)}) %all-to-all-start.2) | async-done | bytes 1048608 | tf_op jit(solution)/shard_map/all_to_all | solution.py:18
  77.2 4.5 %gather_fusion = f32[512]{0:T(512)S(1)} fusion(f32[512,512]{1,0:T(8,128)S(1)} %bitcast.144, s32[512]{0:T(512)S(1)} %bitcast.143), kind=kCustom, calls=%fused_computation | custom fusion | bytes 8192 | tf_op jit(solution)/shard_map/jit(diagonal)/cond/branch_0_fun/gather | solution.py:95
  81.8 1.9 select_subtract_fusion.1
  83.6 3.6 %fusion.6 = f32[512,512]{1,0:T(8,128)S(1)} fusion(f32[512,512]{0,1:T(8,128)S(1)} %select_subtract_fusion.1, f32[512]{0:T(512)S(1)} %gather_fusion), kind=kOutput, calls=%fused_computation.24 | convolution fusion | flops 1611399168 | bytes 2099200 | tf_op jit(solution)/shard_map/dot_general | solution.py:97
  87.2 3.5 %select_subtract_fusion = f32[512,512]{0,1:T(8,128)S(1)} fusion(f32[512,512]{1,0:T(8,128)S(1)} %fusion.6, f32[64,8,512]{2,1,0:T(8,128)S(1)} %all-to-all-done.2), kind=kOutput, calls=%fused_computation.11 | convolution fusion | flops 1611399168 | bytes 3145728 | tf_op jit(solution)/shard_map/dot_general | solution.py:97
  90.7 1.9 fusion.43
  94.6 45.0 %all-gather.3.cloned.1.call-done = bf16[8,2,192,512]{3,2,1,0:T(8,128)(2,1)} async-done(((bf16[1,2,192,512]{3,2,1,0:T(8,128)(2,1)}), bf16[8,2,192,512]{3,2,1,0:T(8,128)(2,1)}) %all-gather.3.cloned.1.call-update) | async-done | bytes 3145744 | tf_op jit(solution)/shard_map/all_gather | solution.py:43
  139.6 2.1 slice_bitcast_fusion.1
  145.8 44.9 %all-gather.5.cloned.1.call-done = bf16[4,8,192,512]{3,2,0,1:T(8,128)(2,1)} async-done(((bf16[4,1,192,512]{3,2,0,1:T(8,128)(2,1)}), bf16[4,8,192,512]{3,2,0,1:T(8,128)(2,1)}) %all-gather.5.cloned.1.call-update) | async-done | bytes 6291472 | tf_op jit(solution)/shard_map/all_gather | solution.py:43
  190.8 3.4 %fusion.40 = (bf16[2,8,192,512]{3,2,0,1:T(8,128)(2,1)S(1)}, bf16[2,8,192,512]{3,2,0,1:T(8,128)(2,1)S(1)}) fusion(bf16[4,8,192,512]{3,2,0,1:T(8,128)(2,1)} %all-gather.5.cloned.1.call-done), kind=kLoop, calls=%fused_computation.73 | loop fusion | bytes 12582912 | tf_op jit(solution)/shard_map/split | solution.py:44
  194.1 1.8 copy.29
  195.9 1.9 fusion.1
  197.8 2.4 reshape.205
  200.2 1.8 copy.28
  203.0 1.4 reshape.203
  204.5 2.0 convolution_convert_fusion.4
  206.5 3.1 %collective-permute-start = (bf16[2,1,512,512]{3,2,1,0:T(8,128)(2,1)S(1)}, bf16[2,1,512,512]{3,2,1,0:T(8,128)(2,1)}, u32[]{:S(2)}, u32[]{:S(2)}) collective-permute-start(bf16[2,1,512,512]{3,2,1,0:T(8,128)(2,1)S(1)} %constant_dynamic-slice_fusion), channel_id=1, source_target_pairs={{0,64},{64,0},{128,192},{192,128},{256,320},{320,256},{384,448},{4... | collective-permute-start | bytes 3145736 | tf_op jit(solution)/shard_map/ppermute | solution.py:48
  209.6 23.3 %collective-permute-done = bf16[2,1,512,512]{3,2,1,0:T(8,128)(2,1)} collective-permute-done((bf16[2,1,512,512]{3,2,1,0:T(8,128)(2,1)S(1)}, bf16[2,1,512,512]{3,2,1,0:T(8,128)(2,1)}, u32[]{:S(2)}, u32[]{:S(2)}) %collective-permute-start) | collective-permute-done | bytes 1048608 | tf_op jit(solution)/shard_map/ppermute | solution.py:48
  233.0 2.5 %fusion.5 = bf16[1,2,1,512,512]{4,3,2,1,0:T(8,128)(2,1)} fusion(bf16[2,1,512,512]{3,2,1,0:T(8,128)(2,1)} %collective-permute-done, bf16[2,2,512,512]{3,2,1,0:T(8,128)(2,1)S(1)} %convolution_convert_fusion.4, s32[]{:T(128)S(6)} %select_n.76), kind=kLoop, calls=%fused_computation.21 | loop fusion | flops 2097152 | bytes 3145732 | tf_op jit(solution)/shard_map/broadcast_in_dim | solution.py:137
  (41 shorter events, 10.4 us)
Async XLA Ops:
  8.1 16.6 %all-to-all-start.1 = ((bf16[8,64,192]{2,1,0:T(8,128)(2,1)}), bf16[8,64,192]{2,1,0:T(8,128)(2,1)S(1)}, u32[]{:S(2)}, u32[]{:S(2)}) async-start(bf16[8,64,192]{2,1,0:T(8,128)(2,1)} %stack.5), calls=%async_computation.1 | async-start | bytes 524288 | tf_op jit(solution)/shard_map/all_to_all | solution.py:30
  18.2 32.7 %copy-start.1 = (bf16[1,1,1,96,512]{4,3,2,1,0:T(8,128)(2,1)S(1)}, bf16[1,1,1,96,512]{4,3,2,1,0:T(8,128)(2,1)}, u32[]{:S(2)}) copy-start(bf16[1,1,1,96,512]{4,3,2,1,0:T(8,128)(2,1)} %param.18) | copy-start | bytes 294916
  18.2 32.8 %copy-start.2 = (bf16[1,1,1,96,512]{4,3,2,1,0:T(8,128)(2,1)S(1)}, bf16[1,1,1,96,512]{4,3,2,1,0:T(8,128)(2,1)}, u32[]{:S(2)}) copy-start(bf16[1,1,1,96,512]{4,3,2,1,0:T(8,128)(2,1)} %param.19) | copy-start | bytes 294916
  42.2 35.1 %all-to-all-start.2 = ((f32[64,8,512]{2,1,0:T(8,128)}), f32[64,8,512]{2,1,0:T(8,128)S(1)}, u32[]{:S(2)}, u32[]{:S(2)}) async-start(f32[64,8,512]{2,1,0:T(8,128)} %broadcast_in_dim.49), calls=%async_computation.2 | async-start | bytes 2097152 | tf_op jit(solution)/shard_map/all_to_all | solution.py:18
  48.9 90.7 %all-gather.3.cloned.1.call-start = ((), (), s32[]{:S(2)}) async-start(), calls=%async_computation.3 | async-start | bytes 3538944 | tf_op jit(solution)/shard_map/all_gather | solution.py:43
  94.3 96.4 %all-gather.5.cloned.1.call-start = ((), (), s32[]{:S(2)}) async-start(), calls=%async_computation.4 | async-start | bytes 7077888 | tf_op jit(solution)/shard_map/all_gather | solution.py:43
  142.6 0.9 copy-start.3
  202.0 2.5 %copy-start = (bf16[2,2,192,512]{3,2,1,0:T(8,128)(2,1)S(1)}, bf16[2,2,192,512]{3,2,1,0:T(8,128)(2,1)}, u32[]{:S(2)}) copy-start(bf16[2,2,192,512]{3,2,1,0:T(8,128)(2,1)} %reshape.205) | copy-start | bytes 2359300
  206.5 26.5 %collective-permute-start = (bf16[2,1,512,512]{3,2,1,0:T(8,128)(2,1)S(1)}, bf16[2,1,512,512]{3,2,1,0:T(8,128)(2,1)}, u32[]{:S(2)}, u32[]{:S(2)}) collective-permute-start(bf16[2,1,512,512]{3,2,1,0:T(8,128)(2,1)S(1)} %constant_dynamic-slice_fusion), channel_id=1, source_target_pairs={{0,64},{64,0},{128,192},{192,128},{256,320},{320,256},{384,448},{4... | collective-permute-start | bytes 3145736 | tf_op jit(solution)/shard_map/ppermute | solution.py:48
Sparse Core Ops, SparseCore 0:
  94.4 45.1 all-gather.2
  145.9 44.7 all-gather.4
